TPU v7x, 32 devices: a whole 2x2x4 slice. The times are simulated.
32 devices in a mesh: dp: 4 (over y, x), fsdp: 8 (over z, core).
Axes of the slice: x: 2, y: 2, z: 4, core: 2. Of those that a mesh axis runs over, the one named last changes fastest.
Arguments:
- inputs: bfloat16 [4, 16, 3584], P('dp', 'fsdp'), may hold values from -16 to 16
- baseline: bfloat16 [4, 16, 3584], P('dp', 'fsdp'), may hold values from -6 to 6
- cotangent: bfloat16 [4, 16, 3584], P('dp', 'fsdp'), may hold values from -6 to 6
- interval: int32 [4], P('dp'), may hold values from 0 to 7
- pre_gain: float32 [3584], replicated, may hold values from 0.1 to 1.9
- post_gain: float32 [3584], replicated, may hold values from 0.1 to 1.9
- gate_weight: bfloat16 [3584, 14336], P('dp', 'fsdp'), may hold values from -0.09375 to 0.09375
- up_weight: bfloat16 [3584, 14336], P('dp', 'fsdp'), may hold values from -0.09375 to 0.09375
- down_weight: bfloat16 [14336, 3584], P('fsdp', 'dp'), may hold values from -0.046875 to 0.046875
Outputs:
- attribution: float32 [4, 16, 3584], P('dp', 'fsdp')
All inputs are finite; a program needn't handle non-finite values.
Results may differ from a plain program's by a relative error of at most 0.0027.
Values may be sent and summed in bfloat16 or wider, within the bound.
No kernel may reach another device: no remote copies, remote signals or barrier semaphores. Data moves between devices by JAX's collectives and lax.ppermute only.
A program may use at most 128 MiB of HBM per device.

v0:
```python
import math
import jax
import jax.numpy as jnp
from jax import lax
from jax.sharding import PartitionSpec as P

STEPS = 4
TOTAL = 32
epsilon = 1e-06
root_coef = math.sqrt(2.0 / math.pi)


def gelu_parts(argument):
    tangent = jnp.tanh(root_coef * (argument + 0.044715 * argument * argument * argument))
    gelu_value = 0.5 * argument * (1.0 + tangent)
    gelu_slope = 0.5 * (1.0 + tangent) + 0.5 * argument * (1.0 - tangent * tangent) * root_coef * (
        1.0 + 3.0 * 0.044715 * argument * argument
    )
    return (gelu_value, gelu_slope)


def norm_back(grad_in, source, gain):
    scaled = grad_in * gain
    inverse = lax.rsqrt(jnp.mean(source * source, axis=-1, keepdims=True) + epsilon)
    inner_mean = jnp.mean(scaled * source, axis=-1, keepdims=True)
    return inverse * (scaled - source * inverse * inverse * inner_mean)


def per_device(
    inputs, baseline, cotangent, interval, pre_gain, post_gain, gate_weight, up_weight, down_weight
):
    gate_full, up_full = (
        lax.all_gather(gate_weight, "dp", axis=0, tiled=True),
        lax.all_gather(up_weight, "dp", axis=0, tiled=True),
    )
    down_full = lax.all_gather(down_weight, "dp", axis=1, tiled=True)
    own_rows = inputs.shape[1]
    model_width = inputs.shape[2]
    whole_in, whole_base, whole_target = (
        lax.all_gather(inputs, "fsdp", axis=1, tiled=True),
        lax.all_gather(baseline, "fsdp", axis=1, tiled=True),
        lax.all_gather(cotangent, "fsdp", axis=1, tiled=True),
    )
    target_all = whole_target[0].astype(jnp.float32)
    source = whole_in[0].astype(jnp.float32)
    anchor = whole_base[0].astype(jnp.float32)
    offset = source - anchor
    own_source = inputs[0].astype(jnp.float32)
    own_anchor = baseline[0].astype(jnp.float32)
    own_offset = own_source - own_anchor
    summed = jnp.zeros((own_rows, model_width), jnp.float32)
    for step_index in range(STEPS):
        fraction = (interval[0].astype(jnp.float32) * STEPS + (step_index + 0.5)) / TOTAL
        sample_point = anchor + fraction * offset
        inverse = lax.rsqrt(jnp.mean(sample_point * sample_point, axis=-1, keepdims=True) + epsilon)
        normed = (sample_point * inverse * pre_gain).astype(jnp.bfloat16)
        gate_val = jnp.dot(normed, gate_full, preferred_element_type=jnp.float32)
        up_val = jnp.dot(normed, up_full, preferred_element_type=jnp.float32)
        gelu_value, gelu_slope = gelu_parts(gate_val)
        hidden = (gelu_value * up_val).astype(jnp.bfloat16)
        branch = lax.psum(jnp.dot(hidden, down_full, preferred_element_type=jnp.float32), "fsdp")
        branch_grad = norm_back(target_all, branch, post_gain).astype(jnp.bfloat16)
        hidden_grad = jnp.dot(branch_grad, down_full.T, preferred_element_type=jnp.float32)
        gate_grad = (hidden_grad * up_val * gelu_slope).astype(jnp.bfloat16)
        up_grad = (hidden_grad * gelu_value).astype(jnp.bfloat16)
        normed_grad = lax.psum_scatter(
            jnp.dot(gate_grad, gate_full.T, preferred_element_type=jnp.float32)
            + jnp.dot(up_grad, up_full.T, preferred_element_type=jnp.float32),
            "fsdp",
            scatter_dimension=0,
            tiled=True,
        )
        own_point = own_anchor + fraction * own_offset
        summed = summed + norm_back(normed_grad, own_point, pre_gain)
    return (own_offset * summed / STEPS)[None]


def solution(mesh):
    return jax.shard_map(
        per_device,
        mesh=mesh,
        in_specs=(
            P("dp", "fsdp", None),
            P("dp", "fsdp", None),
            P("dp", "fsdp", None),
            P("dp"),
            P(),
            P(),
            P("dp", "fsdp"),
            P("dp", "fsdp"),
            P("fsdp", "dp"),
        ),
        out_specs=P("dp", "fsdp", None),
        check_vma=False,
    )
```

profile of v0, /device:TPU:0, one launch (start us, length us, event | category | flops | bytes accessed | tf_op | source)
XLA Modules:
  0.0 617.1 jit_solution(8745663518771204632)
XLA Ops:
  6.5 0.7 all-gather.4.cloned.1.call-update
  7.3 0.0 all-gather.6.cloned.1.call-start
  7.3 0.7 all-gather.6.cloned.1.call-update
  8.0 0.0 all-gather.8.cloned.1.call-start
  8.1 0.7 all-gather.8.cloned.1.call-update
  8.7 0.0 all-reduce.11.cloned.1.call-start
  9.4 0.7 copy.10
  10.2 16.0 %all_gather.18 = bf16[1,16,3584]{2,0,1:T(2,128)(2,1)S(1)} all-gather(bf16[1,2,3584]{2,0,1:T(2,128)(2,1)S(1)} %copy.10), channel_id=1, replica_groups=mesh['dp'=4,'fsdp'=8] {'fsdp'}, dimensions={1}, use_global_device_ids=true | all-gather | bytes 129024 | tf_op jit(solution)/shard_map/all_gather | solution.py:41
  26.1 0.2 convert_element_type.130
  26.4 0.7 copy.11
  27.1 14.1 %all_gather.19 = bf16[1,16,3584]{2,0,1:T(2,128)(2,1)S(1)} all-gather(bf16[1,2,3584]{2,0,1:T(2,128)(2,1)S(1)} %copy.11), channel_id=1, replica_groups=mesh['dp'=4,'fsdp'=8] {'fsdp'}, dimensions={1}, use_global_device_ids=true | all-gather | bytes 129024 | tf_op jit(solution)/shard_map/all_gather | solution.py:40
  41.3 0.3 multiply_reduce_fusion.1
  41.5 0.9 multiply_convert_fusion
  42.4 94.1 %all-gather.4.cloned.1.call-done = bf16[3584,1792]{1,0:T(8,128)(2,1)} async-done(((bf16[896,1792]{1,0:T(8,128)(2,1)}), bf16[3584,1792]{1,0:T(8,128)(2,1)}) %all-gather.4.cloned.1.call-update) | async-done | bytes 12845072 | tf_op jit(solution)/shard_map/all_gather | solution.py:33
  136.5 6.4 %fusion.162 = f32[16,1792]{1,0:T(8,128)S(1)} fusion(bf16[16,3584]{1,0:T(8,128)(2,1)S(1)} %get-tuple-element.35, bf16[3584,1792]{1,0:T(8,128)(2,1)} %all-gather.4.cloned.1.call-done), kind=kOutput, calls=%fused_computation.234 | convolution fusion | flops 205520896 | bytes 13074432 | tf_op jit(solution)/shard_map/dot_general | solution.py:57
  142.9 120.0 %all-gather.6.cloned.1.call-done = bf16[3584,1792]{1,0:T(8,128)(2,1)} async-done(((bf16[896,1792]{1,0:T(8,128)(2,1)}), bf16[3584,1792]{1,0:T(8,128)(2,1)}) %all-gather.6.cloned.1.call-update) | async-done | bytes 12845072 | tf_op jit(solution)/shard_map/all_gather | solution.py:34
  262.9 6.6 %fusion.163 = f32[16,1792]{1,0:T(8,128)S(1)} fusion(bf16[16,3584]{1,0:T(8,128)(2,1)S(1)} %get-tuple-element.35, bf16[3584,1792]{1,0:T(8,128)(2,1)} %all-gather.6.cloned.1.call-done), kind=kOutput, calls=%fused_computation.235 | convolution fusion | flops 205520896 | bytes 13074432 | tf_op jit(solution)/shard_map/dot_general | solution.py:58
  269.5 0.0 slice-start.8
  269.5 0.0 slice-start.9
  269.5 8.6 %fusion.160 = f32[16,1792]{1,0:T(8,128)S(1)} fusion(bf16[16,3584]{1,0:T(8,128)(2,1)S(1)} %get-tuple-element.37, bf16[3584,1792]{1,0:T(8,128)(2,1)} %all-gather.4.cloned.1.call-done), kind=kOutput, calls=%fused_computation.232 | convolution fusion | flops 205520896 | bytes 13074432 | tf_op jit(solution)/shard_map/dot_general | solution.py:57
  278.1 0.0 slice-done.2
  278.2 0.0 slice-start.10
  278.2 0.0 slice-start.11
  278.2 1.8 fusion.161
  280.0 1.2 slice-done.9
  281.2 1.2 slice-done.10
  282.3 1.8 fusion.158
  284.1 1.8 fusion.159
  285.9 1.8 fusion.157
  287.6 13.2 %fusion.156 = f32[16,1792]{1,0:T(8,128)S(1)} fusion(bf16[16,3584]{1,0:T(8,128)(2,1)S(1)} %get-tuple-element.38, bf16[3584,1792]{1,0:T(8,128)(2,1)S(1)} %bitcast.186), kind=kOutput, calls=%fused_computation.228 | convolution fusion | flops 205520896 | bytes 13074432 | tf_op jit(solution)/shard_map/dot_general | solution.py:57
  300.8 88.6 %all-gather.8.cloned.1.call-done = bf16[1792,3584]{1,0:T(8,128)(2,1)} async-done(((bf16[1792,896]{1,0:T(8,128)(2,1)}), bf16[1792,3584]{1,0:T(8,128)(2,1)}) %all-gather.8.cloned.1.call-update) | async-done | bytes 12845072 | tf_op jit(solution)/shard_map/all_gather | solution.py:36
  389.4 7.3 %fusion.75 = f32[16,3584]{1,0:T(8,128)} fusion(bf16[1792,3584]{1,0:T(8,128)(2,1)} %all-gather.8.cloned.1.call-done, f32[16,1792]{1,0:T(8,128)S(1)} %fusion.163, f32[16,1792]{1,0:T(8,128)S(1)} %fusion.162), kind=kOutput, calls=%fused_computation.113 | convolution fusion | flops 205807616 | bytes 13303808 | tf_op jit(solution)/shard_map/dot_general | solution.py:61
  396.7 1.1 copy-done
  397.8 2.5 fusion.74
  400.2 2.5 fusion.73
  402.7 2.5 fusion.72
  405.1 0.0 all-reduce.11.cloned.1.call-update
  405.2 0.0 all-reduce.9.cloned.1.call-start
  405.3 14.3 %all_gather.23 = bf16[1,16,3584]{2,0,1:T(2,128)(2,1)S(1)} all-gather(bf16[1,2,3584]{2,0,1:T(2,128)(2,1)S(1)} %copy.13), channel_id=1, replica_groups=mesh['dp'=4,'fsdp'=8] {'fsdp'}, dimensions={1}, use_global_device_ids=true | all-gather | bytes 129024 | tf_op jit(solution)/shard_map/all_gather | solution.py:42
  419.6 44.6 %all-reduce.11.cloned.1.call-done = (f32[16,3584]{1,0:T(8,128)}, f32[16,3584]{1,0:T(8,128)}, f32[16,3584]{1,0:T(8,128)}, f32[16,3584]{1,0:T(8,128)}) async-done(((f32[16,3584]{1,0:T(8,128)}, f32[16,3584]{1,0:T(8,128)}, f32[16,3584]{1,0:T(8,128)}, f32[16,3584]{1,0:T(8,128)}), (f32[16,3584]{1,0:T(8,128)}, f32[16,3584]{1,0:T(8,128)}, f32[16,3584]{1,0:T(8,128)}, ...) | async-done | bytes 917520 | tf_op jit(solution)/shard_map/psum | solution.py:61
  464.2 1.1 multiply_reduce_fusion
  465.4 1.4 multiply_reduce_fusion.2
  466.9 0.0 slice-start.5
  466.9 0.0 slice-start.6
  466.9 8.3 %fusion.48 = f32[16,1792]{1,0:T(8,128)S(1)} fusion(bf16[1792,3584]{1,0:T(8,128)(2,1)} %all-gather.8.cloned.1.call-done, f32[16,3584]{1,0:T(8,128)} %get-tuple-element.32, bf16[1,16,3584]{2,1,0:T(8,128)(2,1)S(1)} %get-tuple-element.33, f32[16]{0:T(128)S(1)} %broadcast_multiply_fusion, f32[16]{0:T(128)S(1)} %add_rsqrt_fusion, f32[3584]{0:T(1024)S(1)} %copy-done.4), kind=kOutput, calls=%fused_computation.78 | convolution fusion | flops 205979648 | bytes 13318272 | tf_op jit(solution)/shard_map/dot_general | solution.py:63
  475.2 8.2 %fusion.76 = f32[16,3584]{1,0:T(8,128)S(1)} fusion(bf16[3584,1792]{1,0:T(8,128)(2,1)} %all-gather.4.cloned.1.call-done, f32[16,1792]{1,0:T(8,128)S(1)} %fusion.162, f32[16,1792]{1,0:T(8,128)S(1)} %fusion.48, f32[16,1792]{1,0:T(8,128)S(1)} %fusion.163), kind=kOutput, calls=%fused_computation.114 | convolution fusion | flops 206094336 | bytes 13418496 | tf_op jit(solution)/shard_map/dot_general | solution.py:67
  483.5 0.0 slice-done.6
  483.5 4.1 convolution_add_fusion
  487.6 8.1 %fusion.50 = f32[16,1792]{1,0:T(8,128)S(1)} fusion(bf16[1792,3584]{1,0:T(8,128)(2,1)} %all-gather.8.cloned.1.call-done, f32[16,3584]{1,0:T(8,128)S(1)} %copy-done.3, bf16[1,16,3584]{2,1,0:T(8,128)(2,1)S(1)} %get-tuple-element.33, f32[16]{0:T(128)S(1)} %broadcast_multiply_fusion.1, f32[16]{0:T(128)S(1)} %add_rsqrt_fusion.3, f32[3584]{0:T(1024)S(1)} %copy-done.4), kind=kOutput, calls=%fused_computation.79 | convolution fusion | flops 205979648 | bytes 13318272 | tf_op jit(solution)/shard_map/dot_general | solution.py:63
  495.7 8.1 %fusion.78 = f32[16,3584]{1,0:T(8,128)S(1)} fusion(bf16[3584,1792]{1,0:T(8,128)(2,1)} %all-gather.4.cloned.1.call-done, f32[16,1792]{1,0:T(8,128)S(1)} %fusion.160, f32[16,1792]{1,0:T(8,128)S(1)} %fusion.50, f32[16,1792]{1,0:T(8,128)S(1)} %fusion.161), kind=kOutput, calls=%fused_computation.115 | convolution fusion | flops 206094336 | bytes 13418496 | tf_op jit(solution)/shard_map/dot_general | solution.py:67
  503.8 4.2 convolution_add_fusion.1
  508.0 8.1 %fusion.52 = f32[16,1792]{1,0:T(8,128)S(1)} fusion(bf16[1792,3584]{1,0:T(8,128)(2,1)} %all-gather.8.cloned.1.call-done, f32[16,3584]{1,0:T(8,128)S(1)} %copy-done.2, bf16[1,16,3584]{2,1,0:T(8,128)(2,1)S(1)} %get-tuple-element.33, f32[16]{0:T(128)S(1)} %broadcast_multiply_fusion.2, f32[16]{0:T(128)S(1)} %add_rsqrt_fusion.6, f32[3584]{0:T(1024)S(1)} %copy-done.4), kind=kOutput, calls=%fused_computation.80 | convolution fusion | flops 205979648 | bytes 13318272 | tf_op jit(solution)/shard_map/dot_general | solution.py:63
  516.0 8.3 %fusion.80 = f32[16,3584]{1,0:T(8,128)S(1)} fusion(bf16[3584,1792]{1,0:T(8,128)(2,1)} %all-gather.4.cloned.1.call-done, f32[16,1792]{1,0:T(8,128)S(1)} %fusion.158, f32[16,1792]{1,0:T(8,128)S(1)} %fusion.52, f32[16,1792]{1,0:T(8,128)S(1)} %fusion.159), kind=kOutput, calls=%fused_computation.116 | convolution fusion | flops 206094336 | bytes 13418496 | tf_op jit(solution)/shard_map/dot_general | solution.py:67
  524.3 4.1 convolution_add_fusion.2
  528.5 8.1 %fusion.54 = f32[16,1792]{1,0:T(8,128)S(1)} fusion(bf16[1792,3584]{1,0:T(8,128)(2,1)} %all-gather.8.cloned.1.call-done, f32[16,3584]{1,0:T(8,128)S(1)} %copy-done.1, bf16[1,16,3584]{2,1,0:T(8,128)(2,1)S(1)} %get-tuple-element.33, f32[16]{0:T(128)S(1)} %broadcast_multiply_fusion.3, f32[3584]{0:T(1024)S(1)} %copy-done.4, f32[16]{0:T(128)S(1)} %add_rsqrt_fusion.9), kind=kOutput, calls=%fused_computation.81 | convolution fusion | flops 205979648 | bytes 13318272 | tf_op jit(solution)/shard_map/dot_general | solution.py:63
  536.5 0.0 copy-start.6
  536.6 0.0 copy-start.7
  536.6 8.1 %fusion.82 = f32[16,3584]{1,0:T(8,128)S(1)} fusion(bf16[3584,1792]{1,0:T(8,128)(2,1)} %all-gather.4.cloned.1.call-done, f32[16,1792]{1,0:T(8,128)S(1)} %fusion.156, f32[16,1792]{1,0:T(8,128)S(1)} %fusion.54, f32[16,1792]{1,0:T(8,128)S(1)} %fusion.157), kind=kOutput, calls=%fused_computation.117 | convolution fusion | flops 206094336 | bytes 13418496 | tf_op jit(solution)/shard_map/dot_general | solution.py:67
  544.7 4.1 convolution_add_fusion.3
  548.8 0.0 all-reduce.9.cloned.1.call-update
  548.8 0.6 dynamic-slice
  550.1 56.7 %all-reduce.9.cloned.1.call-done = (f32[16,3584]{1,0:T(8,128)}, f32[16,3584]{1,0:T(8,128)}, f32[16,3584]{1,0:T(8,128)}, f32[16,3584]{1,0:T(8,128)}) async-done(((f32[16,3584]{1,0:T(8,128)}, f32[16,3584]{1,0:T(8,128)}, f32[16,3584]{1,0:T(8,128)}, f32[16,3584]{1,0:T(8,128)}), (f32[16,3584]{1,0:T(8,128)}, f32[16,3584]{1,0:T(8,128)}, f32[16,3584]{1,0:T(8,128)}, ...) | async-done | bytes 917520
  606.8 1.5 multiply_reduce_fusion.14
  608.3 1.9 multiply_bitcast_fusion
  (54 shorter events, 0.2 us)
Async XLA Ops:
  6.5 130.0 %all-gather.4.cloned.1.call-start = ((), (), s32[]{:S(2)}) async-start(), calls=%async_computation | async-start | bytes 16056320 | tf_op jit(solution)/shard_map/all_gather | solution.py:33
  7.3 255.7 %all-gather.6.cloned.1.call-start = ((), (), s32[]{:S(2)}) async-start(), calls=%async_computation.1 | async-start | bytes 16056320 | tf_op jit(solution)/shard_map/all_gather | solution.py:34
  8.0 381.4 %all-gather.8.cloned.1.call-start = ((), (), s32[]{:S(2)}) async-start(), calls=%async_computation.2 | async-start | bytes 16056320 | tf_op jit(solution)/shard_map/all_gather | solution.py:36
  8.7 455.5 %all-reduce.11.cloned.1.call-start = ((), (), s32[]{:S(2)}) async-start(), calls=%async_computation.4 | async-start | bytes 1835008 | tf_op jit(solution)/shard_map/psum | solution.py:61
  262.9 15.2 %slice-start = ((s8[12845056]{0:T(1024)(128)(4,1)}), s8[4194304]{0:T(1024)(128)(4,1)S(1)}, s32[]{:S(2)}) async-start(s8[12845056]{0:T(1024)(128)(4,1)} %bitcast.181), calls=%async_computation.5 | async-start | bytes 8388608
  262.9 15.2 %slice-start.1 = ((s8[12845056]{0:T(1024)(128)(4,1)}), s8[4194304]{0:T(1024)(128)(4,1)S(1)}, s32[]{:S(2)}) async-start(s8[12845056]{0:T(1024)(128)(4,1)} %bitcast.181), calls=%async_computation.6 | async-start | bytes 8388608
  269.5 8.6 %slice-start.2 = ((s8[12845056]{0:T(1024)(128)(4,1)}), s8[4194304]{0:T(1024)(128)(4,1)S(1)}, s32[]{:S(2)}) async-start(s8[12845056]{0:T(1024)(128)(4,1)} %bitcast.181), calls=%async_computation.7 | async-start | bytes 8388608
  269.5 8.7 %slice-start.3 = ((s8[12845056]{0:T(1024)(128)(4,1)}), s8[262144]{0:T(1024)(128)(4,1)S(1)}, s32[]{:S(2)}) async-start(s8[12845056]{0:T(1024)(128)(4,1)} %bitcast.181), calls=%async_computation.8 | async-start | bytes 524288
  269.5 10.5 %slice-start.8 = ((s8[12845056]{0:T(1024)(128)(4,1)}), s8[4194304]{0:T(1024)(128)(4,1)S(1)}, s32[]{:S(2)}) async-start(s8[12845056]{0:T(1024)(128)(4,1)} %bitcast.185), calls=%async_computation.13 | async-start | bytes 8388608
  269.5 11.7 %slice-start.9 = ((s8[12845056]{0:T(1024)(128)(4,1)}), s8[4194304]{0:T(1024)(128)(4,1)S(1)}, s32[]{:S(2)}) async-start(s8[12845056]{0:T(1024)(128)(4,1)} %bitcast.185), calls=%async_computation.14 | async-start | bytes 8388608
  278.2 4.2 slice-start.10
  278.2 4.2 slice-start.11
  389.4 8.4 %copy-start = (bf16[1792,3584]{1,0:T(8,128)(2,1)S(1)}, bf16[1792,3584]{1,0:T(8,128)(2,1)}, u32[]{:S(2)}) copy-start(bf16[1792,3584]{1,0:T(8,128)(2,1)} %all-gather.8.cloned.1.call-done) | copy-start | bytes 38535172
  402.7 2.5 copy-start.8
  402.7 61.5 %copy-start.4 = (f32[3584]{0:T(1024)S(1)}, f32[3584]{0:T(1024)}, u32[]{:S(2)}) copy-start(f32[3584]{0:T(1024)} %param.14) | copy-start | bytes 43012
  405.1 78.3 %slice-start.4 = ((s8[12845056]{0:T(1024)(128)(4,1)}), s8[262144]{0:T(1024)(128)(4,1)S(1)}, s32[]{:S(2)}) async-start(s8[12845056]{0:T(1024)(128)(4,1)} %bitcast.183), calls=%async_computation.9 | async-start | bytes 524288
  405.2 201.6 %all-reduce.9.cloned.1.call-start = ((), (), s32[]{:S(2)}) async-start(), calls=%async_computation.3 | async-start | bytes 1835008
  466.9 16.6 %slice-start.5 = ((s8[12845056]{0:T(1024)(128)(4,1)}), s8[4194304]{0:T(1024)(128)(4,1)S(1)}, s32[]{:S(2)}) async-start(s8[12845056]{0:T(1024)(128)(4,1)} %bitcast.183), calls=%async_computation.10 | async-start | bytes 8388608
  466.9 16.6 %slice-start.6 = ((s8[12845056]{0:T(1024)(128)(4,1)}), s8[4194304]{0:T(1024)(128)(4,1)S(1)}, s32[]{:S(2)}) async-start(s8[12845056]{0:T(1024)(128)(4,1)} %bitcast.183), calls=%async_computation.11 | async-start | bytes 8388608
  475.2 8.3 %slice-start.7 = ((s8[12845056]{0:T(1024)(128)(4,1)}), s8[4194304]{0:T(1024)(128)(4,1)S(1)}, s32[]{:S(2)}) async-start(s8[12845056]{0:T(1024)(128)(4,1)} %bitcast.183), calls=%async_computation.12 | async-start | bytes 8388608
  475.2 12.4 %copy-start.3 = (f32[16,3584]{1,0:T(8,128)S(1)}, f32[16,3584]{1,0:T(8,128)}, u32[]{:S(2)}) copy-start(f32[16,3584]{1,0:T(8,128)} %get-tuple-element.31) | copy-start | bytes 688132
  495.7 12.3 %copy-start.2 = (f32[16,3584]{1,0:T(8,128)S(1)}, f32[16,3584]{1,0:T(8,128)}, u32[]{:S(2)}) copy-start(f32[16,3584]{1,0:T(8,128)} %get-tuple-element.30) | copy-start | bytes 688132
  516.0 12.4 %copy-start.1 = (f32[16,3584]{1,0:T(8,128)S(1)}, f32[16,3584]{1,0:T(8,128)}, u32[]{:S(2)}) copy-start(f32[16,3584]{1,0:T(8,128)} %get-tuple-element.29) | copy-start | bytes 688132
  536.5 12.3 %copy-start.9 = (u32[32]{0:T(128)S(1)}, u32[32]{0:T(128)}, u32[]{:S(2)}) copy-start(u32[32]{0:T(128)} %constant.72) | copy-start | bytes 388
  536.5 70.2 %copy-start.5 = (f32[3584]{0:T(1024)S(1)}, f32[3584]{0:T(1024)}, u32[]{:S(2)}) copy-start(f32[3584]{0:T(1024)} %param.13) | copy-start | bytes 43012
  536.5 70.2 %copy-start.6 = (bf16[1,2,3584]{2,1,0:T(2,128)(2,1)S(1)}, bf16[1,2,3584]{2,1,0:T(2,128)(2,1)}, u32[]{:S(2)}) copy-start(bf16[1,2,3584]{2,1,0:T(2,128)(2,1)} %param.10) | copy-start | bytes 43012
  536.6 70.2 %copy-start.7 = (bf16[1,2,3584]{2,1,0:T(2,128)(2,1)S(1)}, bf16[1,2,3584]{2,1,0:T(2,128)(2,1)}, u32[]{:S(2)}) copy-start(bf16[1,2,3584]{2,1,0:T(2,128)(2,1)} %param.9) | copy-start | bytes 43012
Sparse Core Ops, SparseCore 0:
  9.2 127.2 all-gather.3
  138.3 124.5 all-gather.5
  264.8 124.5 all-gather.7
  405.3 58.8 all-reduce.10
  549.0 57.7 all-reduce.8
where the time goes:
time: 627 us; the launch traced here: 617 us
  waiting for transfers between devices  406 us (65%)
  matrix products  138 us (22%)
  blocking collectives  44.4 us (7%)
  between operations  15.1 us (2%)
  other arithmetic  7.36 us (1%)
    all_gather x1, waiting for transfers between devices, per_device(): lax.all_gather(up_weight, 'dp', axis=0, tiled=True)  120 us
    all_gather x1, waiting for transfers between devices, per_device(): lax.all_gather(gate_weight, 'dp', axis=0, tiled=True)  94.1 us
    all_gather x1, waiting for transfers between devices, per_device(): down_full = lax.all_gather(down_weight, 'dp', axis=1, tiled=True)  88.6 us
    unnamed x6, waiting for transfers between devices  58.8 us
    psum x1, waiting for transfers between devices, per_device(): lax.psum(jnp.dot(hidden, down_full, preferred_element_type=jnp.float32),...  44.6 us
    dot_general x4, matrix products, per_device(): jnp.dot(gate_grad, gate_full.T, preferred_element_type=jnp.float32)  32.7 us
    dot_general x4, matrix products, per_device(): jnp.dot(branch_grad, down_full.T, preferred_element_type=jnp.float32)  32.5 us
    dot_general x4, matrix products, per_device(): gate_val = jnp.dot(normed, gate_full, preferred_element_type=jnp.float32)  30 us
  transfers between devices with their start and end apart: 5, of which 5 were waited for; matrix products, arithmetic and copies ran while one was open for 7% of the time, Pallas kernels for 0%

commit v1 on v0

--- a/solution.py
+++ b/solution.py
@@ -33,7 +33,7 @@
         lax.all_gather(gate_weight, "dp", axis=0, tiled=True),
         lax.all_gather(up_weight, "dp", axis=0, tiled=True),
     )
-    down_full = lax.all_gather(down_weight, "dp", axis=1, tiled=True)
+    down_full = jnp.concatenate(lax.all_gather(down_weight, "dp"), axis=1)
     own_rows = inputs.shape[1]
     model_width = inputs.shape[2]
     whole_in, whole_base, whole_target = (

time: 627 us -> 665 us (1.061)
  waiting for transfers between devices: 406 us -> 425 us
  local copies, waits for them, and re-layouts: 5.67 us -> 22.8 us
  matrix products: 138 us -> 147 us
    reshape x0 -> x1, local copies, waits for them, and re-layouts: none -> 18.9 us  [per_device(): down_full = jnp.concatenate(lax.all_gather(down_weight, 'dp'), axis=1)]
    dot_general x4, matrix products: 32.5 us -> 17 us  [per_device(): jnp.dot(branch_grad, down_full.T, preferred_element_type=jnp.float32)]
    dot_general x4, matrix products: 11.9 us -> 25.8 us  [per_device(): up_val = jnp.dot(normed, up_full, preferred_element_type=jnp.float32)]
    dot_general x4, matrix products: 14.7 us -> 28.4 us  [per_device(): jnp.dot(hidden, down_full, preferred_element_type=jnp.float32)]
    all_gather x1, waiting for transfers between devices: 94.1 us -> 108 us  [per_device(): lax.all_gather(gate_weight, 'dp', axis=0, tiled=True)]
  transfers between devices with their start and end apart: 5 -> 5, of which waited for: 5 -> 5; matrix products, arithmetic and copies ran while one was open for 7% -> 4% of each run, Pallas kernels for 0% -> 0%
where the time goes in v1:
time: 665 us; the launch traced here: 661 us
  waiting for transfers between devices  425 us (64%)
  matrix products  147 us (22%)
  blocking collectives  44.4 us (7%)
  local copies, waits for them, and re-layouts  22.8 us (3%)
  between operations  15 us (2%)
  other arithmetic  7.39 us (1%)
    all_gather x1, waiting for transfers between devices, per_device(): lax.all_gather(up_weight, 'dp', axis=0, tiled=True)  120 us
    all_gather x1, waiting for transfers between devices, per_device(): lax.all_gather(gate_weight, 'dp', axis=0, tiled=True)  108 us
    all_gather x1, waiting for transfers between devices, per_device(): down_full = jnp.concatenate(lax.all_gather(down_weight, 'dp'), axis=1)  94.1 us
    unnamed x6, waiting for transfers between devices  58.8 us
    psum x1, waiting for transfers between devices, per_device(): lax.psum(jnp.dot(hidden, down_full, preferred_element_type=jnp.float32),...  44.5 us
    dot_general x4, matrix products, per_device(): jnp.dot(gate_grad, gate_full.T, preferred_element_type=jnp.float32)  33.1 us
    dot_general x4, matrix products, per_device(): jnp.dot(hidden, down_full, preferred_element_type=jnp.float32)  28.4 us
    dot_general x4, matrix products, per_device(): up_val = jnp.dot(normed, up_full, preferred_element_type=jnp.float32)  25.8 us
  transfers between devices with their start and end apart: 5, of which 5 were waited for; matrix products, arithmetic and copies ran while one was open for 4% of the time, Pallas kernels for 0%

profile of v1, /device:TPU:0, one launch (start us, length us, event | category | flops | bytes accessed | tf_op | source)
XLA Modules:
  0.0 661.3 jit_solution(13318239830308574954)
XLA Ops:
  6.5 0.7 all-gather.9.cloned.1.call-update
  7.3 0.0 all-gather.5.cloned.1.call-start
  7.3 0.7 all-gather.5.cloned.1.call-update
  8.0 0.0 all-gather.7.cloned.1.call-start
  8.1 0.7 all-gather.7.cloned.1.call-update
  8.7 0.0 all-reduce.11.cloned.1.call-start
  9.4 0.7 copy.11
  10.2 16.0 %all_gather.21 = bf16[1,16,3584]{2,0,1:T(2,128)(2,1)S(1)} all-gather(bf16[1,2,3584]{2,0,1:T(2,128)(2,1)S(1)} %copy.11), channel_id=1, replica_groups=mesh['dp'=4,'fsdp'=8] {'fsdp'}, dimensions={1}, use_global_device_ids=true | all-gather | bytes 129024 | tf_op jit(solution)/shard_map/all_gather | solution.py:41
  26.1 0.2 convert_element_type.130
  26.4 0.7 copy.12
  27.1 14.1 %all_gather.22 = bf16[1,16,3584]{2,0,1:T(2,128)(2,1)S(1)} all-gather(bf16[1,2,3584]{2,0,1:T(2,128)(2,1)S(1)} %copy.12), channel_id=1, replica_groups=mesh['dp'=4,'fsdp'=8] {'fsdp'}, dimensions={1}, use_global_device_ids=true | all-gather | bytes 129024 | tf_op jit(solution)/shard_map/all_gather | solution.py:40
  41.3 0.3 multiply_reduce_fusion.1
  41.5 0.9 multiply_convert_fusion
  42.4 94.1 %all-gather.9.cloned.1.call-done = bf16[7168,896]{1,0:T(8,128)(2,1)} async-done(((bf16[1792,896]{1,0:T(8,128)(2,1)}), bf16[7168,896]{1,0:T(8,128)(2,1)}) %all-gather.9.cloned.1.call-update) | async-done | bytes 12845072 | tf_op jit(solution)/shard_map/all_gather | solution.py:36
  136.5 18.9 %copy.14 = bf16[1792,4,896]{0,2,1:T(8,128)(2,1)} copy(bf16[1792,4,896]{2,0,1:T(8,128)(2,1)} %bitcast.197) | data formatting | bytes 25690112 | tf_op jit(solution)/shard_map/reshape | solution.py:36
  155.4 107.5 %all-gather.5.cloned.1.call-done = bf16[3584,1792]{1,0:T(8,128)(2,1)} async-done(((bf16[896,1792]{1,0:T(8,128)(2,1)}), bf16[3584,1792]{1,0:T(8,128)(2,1)}) %all-gather.5.cloned.1.call-update) | async-done | bytes 12845072 | tf_op jit(solution)/shard_map/all_gather | solution.py:33
  262.9 6.4 fusion.156
  269.3 120.0 %all-gather.7.cloned.1.call-done = bf16[3584,1792]{1,0:T(8,128)(2,1)} async-done(((bf16[896,1792]{1,0:T(8,128)(2,1)}), bf16[3584,1792]{1,0:T(8,128)(2,1)}) %all-gather.7.cloned.1.call-update) | async-done | bytes 12845072 | tf_op jit(solution)/shard_map/all_gather | solution.py:34
  389.4 6.6 fusion.157
  395.9 1.7 copy-done
  397.7 4.1 fusion.72
  401.8 6.4 fusion.159
  408.2 6.4 fusion.158
  414.6 4.1 fusion.73
  418.7 6.4 fusion.161
  425.1 6.4 fusion.160
  431.6 16.0 %fusion.74 = f32[16,3584]{1,0:T(8,128)} fusion(bf16[1792,3584]{0,1:T(8,128)(2,1)S(1)} %bitcast.189, f32[16,1792]{1,0:T(8,128)S(1)} %fusion.161, f32[16,1792]{1,0:T(8,128)S(1)} %fusion.160), kind=kOutput, calls=%fused_computation.112 | convolution fusion | flops 205807616 | bytes 13303808 | tf_op jit(solution)/shard_map/dot_general | solution.py:61
  447.6 6.4 fusion.163
  454.0 6.4 fusion.162
  460.4 4.1 fusion.75
  464.6 0.0 all-reduce.11.cloned.1.call-update
  464.6 0.0 all-reduce.9.cloned.1.call-start
  464.6 0.0 copy-done.8
  464.7 14.3 %all_gather.27 = bf16[1,16,3584]{2,0,1:T(2,128)(2,1)S(1)} all-gather(bf16[1,2,3584]{2,0,1:T(2,128)(2,1)S(1)} %copy.15), channel_id=1, replica_groups=mesh['dp'=4,'fsdp'=8] {'fsdp'}, dimensions={1}, use_global_device_ids=true | all-gather | bytes 129024 | tf_op jit(solution)/shard_map/all_gather | solution.py:42
  479.0 44.5 %all-reduce.11.cloned.1.call-done = (f32[16,3584]{1,0:T(8,128)}, f32[16,3584]{1,0:T(8,128)}, f32[16,3584]{1,0:T(8,128)}, f32[16,3584]{1,0:T(8,128)}) async-done(((f32[16,3584]{1,0:T(8,128)}, f32[16,3584]{1,0:T(8,128)}, f32[16,3584]{1,0:T(8,128)}, f32[16,3584]{1,0:T(8,128)}), (f32[16,3584]{1,0:T(8,128)}, f32[16,3584]{1,0:T(8,128)}, f32[16,3584]{1,0:T(8,128)}, ...) | async-done | bytes 917520 | tf_op jit(solution)/shard_map/psum | solution.py:61
  523.5 0.0 copy-done.1
  523.5 1.1 multiply_reduce_fusion
  524.7 1.4 multiply_reduce_fusion.2
  526.2 0.0 slice-start
  526.2 0.0 slice-start.1
  526.2 6.7 %fusion.54 = f32[16,1792]{1,0:T(8,128)S(1)} fusion(bf16[1792,3584]{0,1:T(8,128)(2,1)} %bitcast.185, f32[16,3584]{1,0:T(8,128)} %get-tuple-element.29, bf16[1,16,3584]{2,1,0:T(8,128)(2,1)S(1)} %get-tuple-element.33, f32[16]{0:T(128)S(1)} %broadcast_multiply_fusion.3, f32[3584]{0:T(1024)S(1)} %copy-done.1, f32[16]{0:T(128)S(1)} %add_rsqrt_fusion.9), kind=kOutput, calls=%fused_computation.81 | convolution fusion | flops 205979648 | bytes 13318272 | tf_op jit(solution)/shard_map/dot_general | solution.py:63
  532.9 0.0 slice-start.3
  533.0 0.0 copy-start.3
  533.0 6.6 fusion.52
  539.6 0.0 slice-done.2
  539.6 1.8 fusion.50
  541.5 0.0 slice-start.5
  541.5 0.0 slice-start.6
  541.5 1.8 fusion.48
  543.3 8.8 %fusion.82 = f32[16,3584]{1,0:T(8,128)S(1)} fusion(bf16[3584,1792]{1,0:T(8,128)(2,1)} %all-gather.5.cloned.1.call-done, f32[16,1792]{1,0:T(8,128)S(1)} %fusion.156, f32[16,1792]{1,0:T(8,128)S(1)} %fusion.54, f32[16,1792]{1,0:T(8,128)S(1)} %fusion.157), kind=kOutput, calls=%fused_computation.117 | convolution fusion | flops 206094336 | bytes 13418496 | tf_op jit(solution)/shard_map/dot_general | solution.py:67
  552.1 0.0 slice-done.4
  552.1 0.0 slice-done.6
  552.2 4.1 convolution_add_fusion.3
  556.3 8.1 %fusion.80 = f32[16,3584]{1,0:T(8,128)S(1)} fusion(bf16[3584,1792]{1,0:T(8,128)(2,1)} %all-gather.5.cloned.1.call-done, f32[16,1792]{1,0:T(8,128)S(1)} %fusion.158, f32[16,1792]{1,0:T(8,128)S(1)} %fusion.52, f32[16,1792]{1,0:T(8,128)S(1)} %fusion.159), kind=kOutput, calls=%fused_computation.116 | convolution fusion | flops 206094336 | bytes 13418496 | tf_op jit(solution)/shard_map/dot_general | solution.py:67
  564.4 4.3 convolution_add_fusion.2
  568.7 8.1 %fusion.78 = f32[16,3584]{1,0:T(8,128)S(1)} fusion(bf16[3584,1792]{1,0:T(8,128)(2,1)} %all-gather.5.cloned.1.call-done, f32[16,1792]{1,0:T(8,128)S(1)} %fusion.160, f32[16,1792]{1,0:T(8,128)S(1)} %fusion.50, f32[16,1792]{1,0:T(8,128)S(1)} %fusion.161), kind=kOutput, calls=%fused_computation.115 | convolution fusion | flops 206094336 | bytes 13418496 | tf_op jit(solution)/shard_map/dot_general | solution.py:67
  576.7 4.2 convolution_add_fusion.1
  580.9 8.1 %fusion.76 = f32[16,3584]{1,0:T(8,128)S(1)} fusion(bf16[3584,1792]{1,0:T(8,128)(2,1)} %all-gather.5.cloned.1.call-done, f32[16,1792]{1,0:T(8,128)S(1)} %fusion.162, f32[16,1792]{1,0:T(8,128)S(1)} %fusion.48, f32[16,1792]{1,0:T(8,128)S(1)} %fusion.163), kind=kOutput, calls=%fused_computation.114 | convolution fusion | flops 206094336 | bytes 13418496 | tf_op jit(solution)/shard_map/dot_general | solution.py:67
  589.0 4.1 convolution_add_fusion
  593.1 0.0 all-reduce.9.cloned.1.call-update
  593.2 0.6 dynamic-slice
  594.4 56.7 %all-reduce.9.cloned.1.call-done = (f32[16,3584]{1,0:T(8,128)}, f32[16,3584]{1,0:T(8,128)}, f32[16,3584]{1,0:T(8,128)}, f32[16,3584]{1,0:T(8,128)}) async-done(((f32[16,3584]{1,0:T(8,128)}, f32[16,3584]{1,0:T(8,128)}, f32[16,3584]{1,0:T(8,128)}, f32[16,3584]{1,0:T(8,128)}), (f32[16,3584]{1,0:T(8,128)}, f32[16,3584]{1,0:T(8,128)}, f32[16,3584]{1,0:T(8,128)}, ...) | async-done | bytes 917520
  651.1 1.5 multiply_reduce_fusion.14
  652.7 1.9 multiply_bitcast_fusion
  (46 shorter events, 0.2 us)
Async XLA Ops:
  6.5 130.0 %all-gather.9.cloned.1.call-start = ((), (), s32[]{:S(2)}) async-start(), calls=%async_computation.2 | async-start | bytes 16056320 | tf_op jit(solution)/shard_map/all_gather | solution.py:36
  7.3 255.7 %all-gather.5.cloned.1.call-start = ((), (), s32[]{:S(2)}) async-start(), calls=%async_computation | async-start | bytes 16056320 | tf_op jit(solution)/shard_map/all_gather | solution.py:33
  8.0 381.4 %all-gather.7.cloned.1.call-start = ((), (), s32[]{:S(2)}) async-start(), calls=%async_computation.1 | async-start | bytes 16056320 | tf_op jit(solution)/shard_map/all_gather | solution.py:34
  8.7 514.8 %all-reduce.11.cloned.1.call-start = ((), (), s32[]{:S(2)}) async-start(), calls=%async_computation.4 | async-start | bytes 1835008 | tf_op jit(solution)/shard_map/psum | solution.py:61
  389.4 8.3 %copy-start = (bf16[1792,4,896]{0,2,1:T(8,128)(2,1)S(1)}, bf16[1792,4,896]{0,2,1:T(8,128)(2,1)}, u32[]{:S(2)}) copy-start(bf16[1792,4,896]{0,2,1:T(8,128)(2,1)} %copy.14) | copy-start | bytes 38535172
  454.0 10.7 %copy-start.8 = (bf16[1,2,3584]{2,1,0:T(2,128)(2,1)S(1)}, bf16[1,2,3584]{2,1,0:T(2,128)(2,1)}, u32[]{:S(2)}) copy-start(bf16[1,2,3584]{2,1,0:T(2,128)(2,1)} %param.11) | copy-start | bytes 43012
  454.0 69.5 %copy-start.1 = (f32[3584]{0:T(1024)S(1)}, f32[3584]{0:T(1024)}, u32[]{:S(2)}) copy-start(f32[3584]{0:T(1024)} %param.14) | copy-start | bytes 43012
  464.6 186.5 %all-reduce.9.cloned.1.call-start = ((), (), s32[]{:S(2)}) async-start(), calls=%async_computation.3 | async-start | bytes 1835008
  523.5 9.4 %copy-start.4 = (f32[16,3584]{1,0:T(8,128)S(1)}, f32[16,3584]{1,0:T(8,128)}, u32[]{:S(2)}) copy-start(f32[16,3584]{1,0:T(8,128)} %get-tuple-element.30) | copy-start | bytes 688132
  526.2 13.4 %slice-start = ((s8[12845056]{0:T(1024)(128)(4,1)}), s8[4194304]{0:T(1024)(128)(4,1)S(1)}, s32[]{:S(2)}) async-start(s8[12845056]{0:T(1024)(128)(4,1)} %bitcast.191), calls=%async_computation.5 | async-start | bytes 8388608
  526.2 13.4 %slice-start.1 = ((s8[12845056]{0:T(1024)(128)(4,1)}), s8[4194304]{0:T(1024)(128)(4,1)S(1)}, s32[]{:S(2)}) async-start(s8[12845056]{0:T(1024)(128)(4,1)} %bitcast.191), calls=%async_computation.6 | async-start | bytes 8388608
  532.9 6.6 %slice-start.2 = ((s8[12845056]{0:T(1024)(128)(4,1)}), s8[4194304]{0:T(1024)(128)(4,1)S(1)}, s32[]{:S(2)}) async-start(s8[12845056]{0:T(1024)(128)(4,1)} %bitcast.191), calls=%async_computation.7 | async-start | bytes 8388608
  532.9 6.7 %slice-start.3 = ((s8[12845056]{0:T(1024)(128)(4,1)}), s8[262144]{0:T(1024)(128)(4,1)S(1)}, s32[]{:S(2)}) async-start(s8[12845056]{0:T(1024)(128)(4,1)} %bitcast.191), calls=%async_computation.8 | async-start | bytes 524288
  533.0 6.7 %copy-start.3 = (f32[16,3584]{1,0:T(8,128)S(1)}, f32[16,3584]{1,0:T(8,128)}, u32[]{:S(2)}) copy-start(f32[16,3584]{1,0:T(8,128)} %get-tuple-element.31) | copy-start | bytes 688132
  539.6 1.8 copy-start.2
  541.5 10.7 %slice-start.4 = ((s8[12845056]{0:T(1024)(128)(4,1)}), s8[4194304]{0:T(1024)(128)(4,1)S(1)}, s32[]{:S(2)}) async-start(s8[12845056]{0:T(1024)(128)(4,1)} %bitcast.195), calls=%async_computation.9 | async-start | bytes 8388608
  541.5 10.7 %slice-start.5 = ((s8[12845056]{0:T(1024)(128)(4,1)}), s8[4194304]{0:T(1024)(128)(4,1)S(1)}, s32[]{:S(2)}) async-start(s8[12845056]{0:T(1024)(128)(4,1)} %bitcast.195), calls=%async_computation.10 | async-start | bytes 8388608
  541.5 10.7 %slice-start.6 = ((s8[12845056]{0:T(1024)(128)(4,1)}), s8[4194304]{0:T(1024)(128)(4,1)S(1)}, s32[]{:S(2)}) async-start(s8[12845056]{0:T(1024)(128)(4,1)} %bitcast.195), calls=%async_computation.11 | async-start | bytes 8388608
  543.3 8.9 %slice-start.7 = ((s8[12845056]{0:T(1024)(128)(4,1)}), s8[262144]{0:T(1024)(128)(4,1)S(1)}, s32[]{:S(2)}) async-start(s8[12845056]{0:T(1024)(128)(4,1)} %bitcast.195), calls=%async_computation.12 | async-start | bytes 524288
  580.9 12.3 %copy-start.9 = (u32[32]{0:T(128)S(1)}, u32[32]{0:T(128)}, u32[]{:S(2)}) copy-start(u32[32]{0:T(128)} %constant.72) | copy-start | bytes 388
  580.9 70.2 %copy-start.5 = (f32[3584]{0:T(1024)S(1)}, f32[3584]{0:T(1024)}, u32[]{:S(2)}) copy-start(f32[3584]{0:T(1024)} %param.13) | copy-start | bytes 43012
  580.9 70.2 %copy-start.6 = (bf16[1,2,3584]{2,1,0:T(2,128)(2,1)S(1)}, bf16[1,2,3584]{2,1,0:T(2,128)(2,1)}, u32[]{:S(2)}) copy-start(bf16[1,2,3584]{2,1,0:T(2,128)(2,1)} %param.10) | copy-start | bytes 43012
  580.9 70.2 %copy-start.7 = (bf16[1,2,3584]{2,1,0:T(2,128)(2,1)S(1)}, bf16[1,2,3584]{2,1,0:T(2,128)(2,1)}, u32[]{:S(2)}) copy-start(bf16[1,2,3584]{2,1,0:T(2,128)(2,1)} %param.9) | copy-start | bytes 43012
Sparse Core Ops, SparseCore 0:
  9.2 127.2 all-gather.8
  138.3 124.5 all-gather.4
  264.8 124.5 all-gather.6
  464.7 58.7 all-reduce.10
  593.3 57.7 all-reduce.8
